TPU v7x, 32 devices: a whole 2x2x4 slice. The times are simulated.
32 devices in a mesh: groups: 2 (over y), row: 4 (over z), col: 4 (over x, core).
Axes of the slice: x: 2, y: 2, z: 4, core: 2. Of those that a mesh axis runs over, the one named last changes fastest.
Arguments:
- factors: float32 [8, 1280, 5120], P('groups', 'row', 'col'), parts along dimension 0, may hold values from -1.5 to 1.5, as said below
- right_side: float32 [8, 1280, 96], P(('groups', 'col'), 'row'), parts along dimension 0, may hold values from -6 to 6
Outputs:
- forward: float32 [8, 1280, 96], P(('groups', 'col'), 'row'), parts along dimension 0
- solution: float32 [8, 1280, 96], P(('groups', 'col'), 'row'), parts along dimension 0
There are 2 independent parts, one for each index of `groups`. A program takes and returns all parts, laid end to end along the dimension named above; each array names one. Nothing has to cross between parts.
Inputs may be any that keep to these rules, and one draw needn't show every extreme that they name: `factors`: off the diagonal tiles, the entries are those of L below and of U above. Diagonal tile k holds, strictly below its diagonal, the strictly lower part of the inverse of L's unit lower triangular diagonal tile, and on and above its diagonal the inverse of U's upper triangular diagonal tile.
All inputs are finite; a program needn't handle non-finite values.
Results may differ from a plain program's by a relative error of at most 0.00014.
Values sent between devices are 32-bit elements; how exact they have to be, the bound alone decides.
A program may use at most 128 MiB of HBM per device.

v0:
```python
import jax
import jax.numpy as jnp
from jax import lax
from jax.sharding import PartitionSpec as P

precise = lax.Precision.HIGHEST


def from_behind(block, axis, distance):
    devices = range(lax.axis_size(axis))
    route = [(i - distance, i) for i in devices if i - distance in devices]
    return lax.ppermute(block, axis, route)


def product(left, right):
    return jnp.dot(left, right, preferred_element_type=jnp.float32, precision=precise)


def solve_tile(pieces, inverse):
    own_rows = product(inverse, lax.all_gather(pieces, "row", axis=0, tiled=True))
    full_tile = lax.all_gather(own_rows, "row", axis=0, tiled=True)
    return (own_rows, full_tile)


def sweep_wave(factors, source, inverse, direction, column, tile_count):
    row_count = factors.shape[1]
    tile_size = factors.shape[2]
    portions = 2
    portion = source.shape[1] // portions
    position = column if direction == 1 else tile_count - 1 - column
    flattened = factors.reshape(tile_count * row_count, tile_size)

    def advance(moment, carry):
        outgoing, rows_out = carry
        arrived = from_behind(outgoing, "col", direction)
        batch_index = moment - position
        usable = (batch_index >= 0) & (batch_index < portions)
        offset = jnp.clip(batch_index, 0, portions - 1) * portion
        selected = lax.dynamic_slice_in_dim(source, offset, portion, 1)
        local_sum = lax.dynamic_index_in_dim(arrived, column, 0, keepdims=False)
        own_rows, full_tile = solve_tile(selected - local_sum, inverse)
        updated = arrived + product(flattened, full_tile).reshape(tile_count, row_count, portion)
        placed = lax.dynamic_update_slice_in_dim(rows_out, own_rows, offset, 1)
        rows_out = jnp.where(usable, placed, rows_out)
        return (updated, rows_out)

    starting = (
        jnp.zeros((tile_count, row_count, portion), jnp.float32),
        jnp.zeros(source.shape, jnp.float32),
    )
    return lax.fori_loop(0, tile_count + portions - 1, advance, starting)[1]


def local(factors, right_side):
    tile_count, row_count, tile_size = factors.shape
    column = lax.axis_index("col")
    row_index = lax.axis_index("row")
    diagonal = lax.dynamic_index_in_dim(factors, column, 0, keepdims=False)
    global_rows = row_index * row_count + jnp.arange(row_count)[:, None]
    global_cols = jnp.arange(tile_size)[None, :]
    lower = jnp.where(global_cols < global_rows, diagonal, 0.0) + (
        global_cols == global_rows
    ).astype(jnp.float32)
    upper = jnp.where(global_cols >= global_rows, diagonal, 0.0)
    source = right_side[0]
    forward = sweep_wave(factors, source, lower, 1, column, tile_count)
    solution = sweep_wave(factors, forward, upper, -1, column, tile_count)
    return (forward[None], solution[None])


def solution(mesh):
    return jax.shard_map(
        local,
        mesh=mesh,
        in_specs=(P("groups", "row", "col"), P(("groups", "col"), "row", None)),
        out_specs=(P(("groups", "col"), "row", None), P(("groups", "col"), "row", None)),
        check_vma=False,
    )
```

profile of v0, /device:TPU:0, one launch (start us, length us, event | category | flops | bytes accessed | tf_op | source)
XLA Modules:
  0.0 540.6 jit_solution(1709800131947166748)
XLA Ops:
  3.2 294.6 %while.36 = (s32[]{:T(128)}, f32[4,320,48]{1,0,2:T(4,128)}, f32[320,96]{0,1:T(8,128)}, s32[]{:T(128)}, f32[320,96]{0,1:T(8,128)}, /*index=5*/s32[]{:T(128)}, f32...) while((s32[]{:T(128)}, f32[4,320,48]{1,0,2:T(4,128)}, ...), condition=%wide.region_1.2_spmd.clone, body=%wide.region_0.1_spmd.clone.sunk | while | flops 1179801600 | bytes 14729507 | solution.py:51
  9.8 15.5 %all-gather.12 = f32[4,320,48]{1,2,0:T(8,128)S(1)} all-gather(f32[1,320,48]{1,2,0:T(8,128)S(1)} %fusion.29), channel_id=1, replica_groups=mesh['groups'=2,'row'=4,'col'=4] {'row'}, dimensions={0}, use_global_device_ids=true | all-gather | bytes 307200 | tf_op jit(solution)/shard_map/while/body/eval_jaxpr/all_gather | solution.py:20
  30.4 14.6 %all-gather.13 = f32[4,320,48]{1,2,0:T(8,128)S(1)} all-gather(f32[1,320,48]{1,2,0:T(8,128)S(1)} %bitcast.94), channel_id=1, replica_groups=mesh['groups'=2,'row'=4,'col'=4] {'row'}, dimensions={0}, use_global_device_ids=true | all-gather | bytes 307200 | tf_op jit(solution)/shard_map/while/body/eval_jaxpr/all_gather | solution.py:21
  47.0 9.6 %convolution_bitcast_fusion.4 = f32[1280,48]{0,1:T(8,128)} fusion(f32[1280,48]{0,1:T(8,128)S(1)} %reshape.57, f32[1280,1280]{1,0:T(8,128)} %get-tuple-element.604), kind=kOutput, calls=%fused_computation.clone.1 | convolution fusion | flops 943718400 | bytes 7045120 | tf_op jit(solution)/shard_map/while/body/eval_jaxpr/dot_general | solution.py:16
  66.8 14.0 %all-gather.12 = f32[4,320,48]{1,2,0:T(8,128)S(1)} all-gather(f32[1,320,48]{1,2,0:T(8,128)S(1)} %fusion.29), channel_id=1, replica_groups=mesh['groups'=2,'row'=4,'col'=4] {'row'}, dimensions={0}, use_global_device_ids=true | all-gather | bytes 307200 | tf_op jit(solution)/shard_map/while/body/eval_jaxpr/all_gather | solution.py:20
  85.8 14.1 %all-gather.13 = f32[4,320,48]{1,2,0:T(8,128)S(1)} all-gather(f32[1,320,48]{1,2,0:T(8,128)S(1)} %bitcast.94), channel_id=1, replica_groups=mesh['groups'=2,'row'=4,'col'=4] {'row'}, dimensions={0}, use_global_device_ids=true | all-gather | bytes 307200 | tf_op jit(solution)/shard_map/while/body/eval_jaxpr/all_gather | solution.py:21
  127.0 13.9 %all-gather.12 = f32[4,320,48]{1,2,0:T(8,128)S(1)} all-gather(f32[1,320,48]{1,2,0:T(8,128)S(1)} %fusion.29), channel_id=1, replica_groups=mesh['groups'=2,'row'=4,'col'=4] {'row'}, dimensions={0}, use_global_device_ids=true | all-gather | bytes 307200 | tf_op jit(solution)/shard_map/while/body/eval_jaxpr/all_gather | solution.py:20
  145.9 14.1 %all-gather.13 = f32[4,320,48]{1,2,0:T(8,128)S(1)} all-gather(f32[1,320,48]{1,2,0:T(8,128)S(1)} %bitcast.94), channel_id=1, replica_groups=mesh['groups'=2,'row'=4,'col'=4] {'row'}, dimensions={0}, use_global_device_ids=true | all-gather | bytes 307200 | tf_op jit(solution)/shard_map/while/body/eval_jaxpr/all_gather | solution.py:21
  187.3 14.0 %all-gather.12 = f32[4,320,48]{1,2,0:T(8,128)S(1)} all-gather(f32[1,320,48]{1,2,0:T(8,128)S(1)} %fusion.29), channel_id=1, replica_groups=mesh['groups'=2,'row'=4,'col'=4] {'row'}, dimensions={0}, use_global_device_ids=true | all-gather | bytes 307200 | tf_op jit(solution)/shard_map/while/body/eval_jaxpr/all_gather | solution.py:20
  206.3 14.4 %all-gather.13 = f32[4,320,48]{1,2,0:T(8,128)S(1)} all-gather(f32[1,320,48]{1,2,0:T(8,128)S(1)} %bitcast.94), channel_id=1, replica_groups=mesh['groups'=2,'row'=4,'col'=4] {'row'}, dimensions={0}, use_global_device_ids=true | all-gather | bytes 307200 | tf_op jit(solution)/shard_map/while/body/eval_jaxpr/all_gather | solution.py:21
  248.9 14.0 %all-gather.12 = f32[4,320,48]{1,2,0:T(8,128)S(1)} all-gather(f32[1,320,48]{1,2,0:T(8,128)S(1)} %fusion.29), channel_id=1, replica_groups=mesh['groups'=2,'row'=4,'col'=4] {'row'}, dimensions={0}, use_global_device_ids=true | all-gather | bytes 307200 | tf_op jit(solution)/shard_map/while/body/eval_jaxpr/all_gather | solution.py:20
  268.0 14.5 %all-gather.13 = f32[4,320,48]{1,2,0:T(8,128)S(1)} all-gather(f32[1,320,48]{1,2,0:T(8,128)S(1)} %bitcast.94), channel_id=1, replica_groups=mesh['groups'=2,'row'=4,'col'=4] {'row'}, dimensions={0}, use_global_device_ids=true | all-gather | bytes 307200 | tf_op jit(solution)/shard_map/while/body/eval_jaxpr/all_gather | solution.py:21
  284.5 9.6 %convolution_bitcast_fusion.4 = f32[1280,48]{0,1:T(8,128)} fusion(f32[1280,48]{0,1:T(8,128)S(1)} %reshape.57, f32[1280,1280]{1,0:T(8,128)} %get-tuple-element.604), kind=kOutput, calls=%fused_computation.clone.1 | convolution fusion | flops 943718400 | bytes 7045120 | tf_op jit(solution)/shard_map/while/body/eval_jaxpr/dot_general | solution.py:16
  297.8 242.1 %while.37 = (s32[]{:T(128)}, f32[4,320,48]{1,0,2:T(4,128)S(1)}, f32[320,96]{0,1:T(8,128)S(1)}, s32[]{:T(128)}, f32[320,96]{0,1:T(8,128)}, /*index=5*/s32[]{:T(12...) while((s32[]{:T(128)}, f32[4,320,48]{1,0,2:T(4,128)S(1)}, ...), condition=%wide.region_3.4_spmd.clone, body=%wide.region_2.3_spmd.clone.sunk | while | flops 1179801600 | bytes 14741795 | solution.py:51
  307.3 14.0 %all-gather.14 = f32[4,320,48]{1,2,0:T(8,128)S(1)} all-gather(f32[1,320,48]{1,2,0:T(8,128)S(1)} %fusion.35), channel_id=1, replica_groups=mesh['groups'=2,'row'=4,'col'=4] {'row'}, dimensions={0}, use_global_device_ids=true | all-gather | bytes 307200 | tf_op jit(solution)/shard_map/while/body/eval_jaxpr/all_gather | solution.py:20
  323.1 14.6 %all-gather.15 = f32[4,320,48]{1,2,0:T(8,128)S(1)} all-gather(f32[1,320,48]{1,2,0:T(8,128)S(1)} %bitcast.95), channel_id=1, replica_groups=mesh['groups'=2,'row'=4,'col'=4] {'row'}, dimensions={0}, use_global_device_ids=true | all-gather | bytes 307200 | tf_op jit(solution)/shard_map/while/body/eval_jaxpr/all_gather | solution.py:21
  357.6 14.1 %all-gather.14 = f32[4,320,48]{1,2,0:T(8,128)S(1)} all-gather(f32[1,320,48]{1,2,0:T(8,128)S(1)} %fusion.35), channel_id=1, replica_groups=mesh['groups'=2,'row'=4,'col'=4] {'row'}, dimensions={0}, use_global_device_ids=true | all-gather | bytes 307200 | tf_op jit(solution)/shard_map/while/body/eval_jaxpr/all_gather | solution.py:20
  373.5 14.0 %all-gather.15 = f32[4,320,48]{1,2,0:T(8,128)S(1)} all-gather(f32[1,320,48]{1,2,0:T(8,128)S(1)} %bitcast.95), channel_id=1, replica_groups=mesh['groups'=2,'row'=4,'col'=4] {'row'}, dimensions={0}, use_global_device_ids=true | all-gather | bytes 307200 | tf_op jit(solution)/shard_map/while/body/eval_jaxpr/all_gather | solution.py:21
  405.8 14.5 %all-gather.14 = f32[4,320,48]{1,2,0:T(8,128)S(1)} all-gather(f32[1,320,48]{1,2,0:T(8,128)S(1)} %fusion.35), channel_id=1, replica_groups=mesh['groups'=2,'row'=4,'col'=4] {'row'}, dimensions={0}, use_global_device_ids=true | all-gather | bytes 307200 | tf_op jit(solution)/shard_map/while/body/eval_jaxpr/all_gather | solution.py:20
  422.2 14.0 %all-gather.15 = f32[4,320,48]{1,2,0:T(8,128)S(1)} all-gather(f32[1,320,48]{1,2,0:T(8,128)S(1)} %bitcast.95), channel_id=1, replica_groups=mesh['groups'=2,'row'=4,'col'=4] {'row'}, dimensions={0}, use_global_device_ids=true | all-gather | bytes 307200 | tf_op jit(solution)/shard_map/while/body/eval_jaxpr/all_gather | solution.py:21
  453.1 14.6 %all-gather.14 = f32[4,320,48]{1,2,0:T(8,128)S(1)} all-gather(f32[1,320,48]{1,2,0:T(8,128)S(1)} %fusion.35), channel_id=1, replica_groups=mesh['groups'=2,'row'=4,'col'=4] {'row'}, dimensions={0}, use_global_device_ids=true | all-gather | bytes 307200 | tf_op jit(solution)/shard_map/while/body/eval_jaxpr/all_gather | solution.py:20
  469.6 14.0 %all-gather.15 = f32[4,320,48]{1,2,0:T(8,128)S(1)} all-gather(f32[1,320,48]{1,2,0:T(8,128)S(1)} %bitcast.95), channel_id=1, replica_groups=mesh['groups'=2,'row'=4,'col'=4] {'row'}, dimensions={0}, use_global_device_ids=true | all-gather | bytes 307200 | tf_op jit(solution)/shard_map/while/body/eval_jaxpr/all_gather | solution.py:21
  500.3 14.1 %all-gather.14 = f32[4,320,48]{1,2,0:T(8,128)S(1)} all-gather(f32[1,320,48]{1,2,0:T(8,128)S(1)} %fusion.35), channel_id=1, replica_groups=mesh['groups'=2,'row'=4,'col'=4] {'row'}, dimensions={0}, use_global_device_ids=true | all-gather | bytes 307200 | tf_op jit(solution)/shard_map/while/body/eval_jaxpr/all_gather | solution.py:20
  516.3 14.0 %all-gather.15 = f32[4,320,48]{1,2,0:T(8,128)S(1)} all-gather(f32[1,320,48]{1,2,0:T(8,128)S(1)} %bitcast.95), channel_id=1, replica_groups=mesh['groups'=2,'row'=4,'col'=4] {'row'}, dimensions={0}, use_global_device_ids=true | all-gather | bytes 307200 | tf_op jit(solution)/shard_map/while/body/eval_jaxpr/all_gather | solution.py:21
  (136 shorter events, 234.9 us)
Async XLA Ops:
  4.0 3.9 collective-permute-start
  62.1 2.8 collective-permute-start
  117.0 8.1 %collective-permute-start = (f32[4,320,48]{1,0,2:T(4,128)}, f32[4,320,48]{1,0,2:T(4,128)}, u32[]{:S(2)}, u32[]{:S(2)}) collective-permute-start(f32[4,320,48]{1,0,2:T(4,128)} %broadcast_select_fusion.4), channel_id=1, source_target_pairs={{0,1},{1,2},{2,3},{4,5},{5,6},{6,7},{8,9},{9,10},{10,11},{12,13},{... | collective-permute-start | bytes 737288 | tf_op jit(solution)/shard_map/while/body/eval_jaxpr/ppermute | solution.py:12
  177.0 8.3 %collective-permute-start = (f32[4,320,48]{1,0,2:T(4,128)}, f32[4,320,48]{1,0,2:T(4,128)}, u32[]{:S(2)}, u32[]{:S(2)}) collective-permute-start(f32[4,320,48]{1,0,2:T(4,128)} %broadcast_select_fusion.4), channel_id=1, source_target_pairs={{0,1},{1,2},{2,3},{4,5},{5,6},{6,7},{8,9},{9,10},{10,11},{12,13},{... | collective-permute-start | bytes 737288 | tf_op jit(solution)/shard_map/while/body/eval_jaxpr/ppermute | solution.py:12
  237.8 9.2 %collective-permute-start = (f32[4,320,48]{1,0,2:T(4,128)}, f32[4,320,48]{1,0,2:T(4,128)}, u32[]{:S(2)}, u32[]{:S(2)}) collective-permute-start(f32[4,320,48]{1,0,2:T(4,128)} %broadcast_select_fusion.4), channel_id=1, source_target_pairs={{0,1},{1,2},{2,3},{4,5},{5,6},{6,7},{8,9},{9,10},{10,11},{12,13},{... | collective-permute-start | bytes 737288 | tf_op jit(solution)/shard_map/while/body/eval_jaxpr/ppermute | solution.py:12
  298.1 8.2 %collective-permute-start.1 = (f32[4,320,48]{1,0,2:T(4,128)S(1)}, f32[4,320,48]{1,0,2:T(4,128)S(1)}, u32[]{:S(2)}, u32[]{:S(2)}) collective-permute-start(f32[4,320,48]{1,0,2:T(4,128)S(1)} %broadcast_select_fusion.5), channel_id=1, source_target_pairs={{1,0},{2,1},{3,2},{5,4},{6,5},{7,6},{9,8},{10,9},{11,10},{13,12},{... | collective-permute-start | bytes 737288 | tf_op jit(solution)/shard_map/while/body/eval_jaxpr/ppermute | solution.py:12
  347.4 9.2 %collective-permute-start.1 = (f32[4,320,48]{1,0,2:T(4,128)S(1)}, f32[4,320,48]{1,0,2:T(4,128)S(1)}, u32[]{:S(2)}, u32[]{:S(2)}) collective-permute-start(f32[4,320,48]{1,0,2:T(4,128)S(1)} %broadcast_select_fusion.5), channel_id=1, source_target_pairs={{1,0},{2,1},{3,2},{5,4},{6,5},{7,6},{9,8},{10,9},{11,10},{13,12},{... | collective-permute-start | bytes 737288 | tf_op jit(solution)/shard_map/while/body/eval_jaxpr/ppermute | solution.py:12
  397.2 7.6 %collective-permute-start.1 = (f32[4,320,48]{1,0,2:T(4,128)S(1)}, f32[4,320,48]{1,0,2:T(4,128)S(1)}, u32[]{:S(2)}, u32[]{:S(2)}) collective-permute-start(f32[4,320,48]{1,0,2:T(4,128)S(1)} %broadcast_select_fusion.5), channel_id=1, source_target_pairs={{1,0},{2,1},{3,2},{5,4},{6,5},{7,6},{9,8},{10,9},{11,10},{13,12},{... | collective-permute-start | bytes 737288 | tf_op jit(solution)/shard_map/while/body/eval_jaxpr/ppermute | solution.py:12
  445.9 6.3 %collective-permute-start.1 = (f32[4,320,48]{1,0,2:T(4,128)S(1)}, f32[4,320,48]{1,0,2:T(4,128)S(1)}, u32[]{:S(2)}, u32[]{:S(2)}) collective-permute-start(f32[4,320,48]{1,0,2:T(4,128)S(1)} %broadcast_select_fusion.5), channel_id=1, source_target_pairs={{1,0},{2,1},{3,2},{5,4},{6,5},{7,6},{9,8},{10,9},{11,10},{13,12},{... | collective-permute-start | bytes 737288 | tf_op jit(solution)/shard_map/while/body/eval_jaxpr/ppermute | solution.py:12
  493.3 6.1 %collective-permute-start.1 = (f32[4,320,48]{1,0,2:T(4,128)S(1)}, f32[4,320,48]{1,0,2:T(4,128)S(1)}, u32[]{:S(2)}, u32[]{:S(2)}) collective-permute-start(f32[4,320,48]{1,0,2:T(4,128)S(1)} %broadcast_select_fusion.5), channel_id=1, source_target_pairs={{1,0},{2,1},{3,2},{5,4},{6,5},{7,6},{9,8},{10,9},{11,10},{13,12},{... | collective-permute-start | bytes 737288 | tf_op jit(solution)/shard_map/while/body/eval_jaxpr/ppermute | solution.py:12
  539.9 0.7 copy-start
where the time goes:
time: 549 us; the launch traced here: 541 us
  blocking collectives  285 us (52%)
  matrix products  115 us (21%)
  local copies, waits for them, and re-layouts  40.6 us (7%)
  waiting for transfers between devices  34.9 us (6%)
  starting transfers between devices  34.6 us (6%)
  other arithmetic  28.5 us (5%)
    all_gather x10, blocking collectives, solve_tile(): lax.all_gather(pieces, 'row', axis=0, tiled=True)  143 us
    all_gather x10, blocking collectives, solve_tile(): full_tile = lax.all_gather(own_rows, 'row', axis=0, tiled=True)  142 us
    dot_general x20, matrix products, product(): jnp.dot(left, right, preferred_element_type=jnp.float32, precision=precise)  115 us
    ppermute x10, waiting for transfers between devices, from_behind(): return lax.ppermute(block, axis, route)  34.9 us
    ppermute x10, starting transfers between devices, from_behind(): return lax.ppermute(block, axis, route)  34.6 us
    while x20, other arithmetic  17 us
    while x20, local copies, waits for them, and re-layouts  14.1 us
  transfers between devices with their start and end apart: 10, of which 10 were waited for; matrix products, arithmetic and copies ran while one was open for 0% of the time, Pallas kernels for 0%

commit v1 on v0

v1 whole, which is shorter than its diff:
```python
import functools

import jax
import jax.numpy as jnp
from jax import lax
from jax.experimental import pallas as pl
from jax.experimental.pallas import tpu as pltpu
from jax.sharding import PartitionSpec as P

MESH = pl.DeviceIdType.MESH
CHUNKS = 3


def kernel(
    n_row, n_col, chunks,
    ahi_hbm, alo_hbm, rs_ref,
    fwd_ref, sol_ref,
    ahi, alo, v_buf, f_buf, w_buf, s_buf, t_buf, tb_buf, rin, rout, rbin, rbout,
    a_sem, v_send, v_recv, f_send, f_recv, w_send, w_recv, s_send, s_recv,
    r_send, r_recv, rb_send, rb_recv, b0_send,
):
    r = lax.axis_index("row")
    c = lax.axis_index("col")
    last = n_col - 1

    def load(i, k):
        return (
            pltpu.make_async_copy(ahi_hbm.at[k], ahi.at[k], a_sem.at[0, k]),
            pltpu.make_async_copy(alo_hbm.at[k], alo.at[k], a_sem.at[1, k]),
        )

    def start_load(i, _):
        k = lax.rem(c + i, n_col + 1)
        for copy in load(i, k):
            copy.start()
        return 0

    lax.fori_loop(0, n_col + 1, start_load, 0)

    def wait_load(k):
        for copy in load(0, k):
            copy.wait()

    barrier = pltpu.get_barrier_semaphore()

    def greet(i, _):
        rr, cc = i // n_col, i % n_col

        @pl.when(i != r * n_col + c)
        def _():
            pl.semaphore_signal(barrier, inc=1, device_id={"row": rr, "col": cc}, device_id_type=MESH)

        return 0

    lax.fori_loop(0, n_row * n_col, greet, 0)
    pl.semaphore_wait(barrier, n_row * n_col - 1)

    def remote(src, dst, send, recv, row, col):
        return pltpu.make_async_remote_copy(
            src_ref=src, dst_ref=dst, send_sem=send, recv_sem=recv,
            device_id={"row": row, "col": col}, device_id_type=MESH,
        )

    def around(d):
        half = (d + 1) // 2
        odd = d % 2
        return lax.rem(r + odd * half - (1 - odd) * half + n_row, n_row)

    def each_chunk(body):
        def step(q, _):
            body(q)
            return 0

        lax.fori_loop(0, chunks, step, 0)

    def each_row(body, first=0):
        def step(d, _):
            body(around(d))
            return 0

        lax.fori_loop(first, n_row, step, 0, unroll=n_row <= 4)

    def part(x, k, s):
        hi = x.astype(jnp.bfloat16)
        lo = (x - hi.astype(jnp.float32)).astype(jnp.bfloat16)
        both = jnp.concatenate([hi, lo], axis=0)
        dims = (((1,), (1,)), ((), ()))
        m = x.shape[0]
        one = lax.dot_general(both, ahi[k, s], dims, preferred_element_type=jnp.float32)
        two = lax.dot_general(hi, alo[k, s], dims, preferred_element_type=jnp.float32)
        return one[:m] + one[m:] + two

    def combine(buf, k, q, wait):
        def step(d, acc):
            s = around(d)
            if wait is not None:
                wait(q, s)
            return acc + part(buf[q, s], k, s)

        zero = jnp.zeros(buf.shape[2:], jnp.float32)
        return lax.fori_loop(0, n_row, step, zero, unroll=n_row <= 4)

    def arrival(buf, recv):
        def wait(q, s):
            remote(buf.at[q, s], buf.at[q, s], recv.at[q, s], recv.at[q, s], r, c).wait_recv()

        return wait

    def arrival_but_own(buf, recv):
        inner = arrival(buf, recv)

        def wait(q, s):
            @pl.when(s != r)
            def _():
                inner(q, s)

        return wait

    def to_row(src, buf, send, recv, q, row):
        return remote(src, buf.at[q, r], send.at[q, row], recv.at[q, r], row, c)

    @pl.when(c == 0)
    def _():
        def one(q):
            v_buf[q, r] = rs_ref[q]
            each_row(lambda row: to_row(rs_ref.at[q], v_buf, v_send, v_recv, q, row).start(), 1)

        each_chunk(one)

    def first_run(q):
        return remote(rs_ref.at[q], rin.at[c, q], r_send.at[c, q], r_recv.at[c, q], r, 0)

    @pl.when(c > 0)
    def _():
        each_chunk(lambda q: first_run(q).start())

    wait_load(c)

    def back_run(q):
        return remote(f_buf.at[q, r], rbin.at[c, q], b0_send.at[q], rb_recv.at[c, q], r, last)

    def solve_forward(wait):
        def one(q):
            acc = combine(v_buf, c, q, wait)
            f_buf[q, r] = acc
            each_row(lambda row: to_row(f_buf.at[q, r], f_buf, f_send, f_recv, q, row).start(), 1)

            @pl.when(c < last)
            def _():
                back_run(q).start()

            fwd_ref[q] = acc

        each_chunk(one)

    @pl.when(c == 0)
    def _():
        solve_forward(arrival_but_own(v_buf, v_recv))

    @pl.when(c > 0)
    def _():
        solve_forward(arrival(v_buf, v_recv))

    def wait_run(run, recv, k, q):
        remote(run.at[k, q], run.at[k, q], recv.at[k, q], recv.at[k, q], r, c).wait_recv()

    def sweep(buf, recv, first, count, step, run_in, run_recv, run_out, run_send, stage, out, send, out_recv):
        nxt = c + step
        wait = arrival_but_own(buf, recv)
        wait_load(first)

        def one(q):
            acc = combine(buf, first, q, wait)
            wait_run(run_in, run_recv, first, q)
            stage[q] = run_in[first, q] - acc
            each_row(
                lambda row: remote(stage.at[q], out.at[q, r], send.at[q, row], out_recv.at[q, r], row, nxt).start()
            )

        each_chunk(one)

        def other(i, _):
            k = first + step * i
            wait_load(k)

            def inner(q):
                acc = combine(buf, k, q, None)
                wait_run(run_in, run_recv, k, q)
                run_out[k, q] = run_in[k, q] - acc
                remote(run_out.at[k, q], run_in.at[k, q], run_send.at[k, q], run_recv.at[k, q], r, nxt).start()

            each_chunk(inner)
            return 0

        lax.fori_loop(1, count, other, 0)

    @pl.when(c < last)
    def _():
        sweep(f_buf, f_recv, c + 1, last - c, 1, rin, r_recv, rout, r_send, t_buf, v_buf, w_send, v_recv)

    wait_load(n_col)

    def solve_backward(buf, wait):
        def one(q):
            acc = combine(buf, n_col, q, wait)
            s_buf[q, r] = acc

            @pl.when(c > 0)
            def _():
                each_row(lambda row: to_row(s_buf.at[q, r], s_buf, s_send, s_recv, q, row).start(), 1)

            sol_ref[q] = acc

        each_chunk(one)

    @pl.when(c == last)
    def _():
        solve_backward(f_buf, arrival_but_own(f_buf, f_recv))

    @pl.when(c < last)
    def _():
        solve_backward(w_buf, arrival(w_buf, w_recv))

    @pl.when(c > 0)
    def _():
        sweep(s_buf, s_recv, c - 1, c, -1, rbin, rb_recv, rbout, rb_send, tb_buf, w_buf, v_send, w_recv)

    def sent(src, send):
        remote(src, src, send, send, r, c).wait_send()

    def finish(q):
        @pl.when(c == 0)
        def _():
            each_row(lambda row: sent(rs_ref.at[q], v_send.at[q, row]), 1)

        @pl.when(c > 0)
        def _():
            sent(rs_ref.at[q], r_send.at[c, q])
            each_row(lambda row: sent(tb_buf.at[q], v_send.at[q, row]))
            each_row(lambda row: sent(s_buf.at[q, r], s_send.at[q, row]), 1)

        each_row(lambda row: sent(f_buf.at[q, r], f_send.at[q, row]), 1)

        @pl.when(c < last)
        def _():
            sent(f_buf.at[q, r], b0_send.at[q])
            each_row(lambda row: sent(t_buf.at[q], w_send.at[q, row]))

        def run(k, _):
            @pl.when(k > c + 1)
            def _():
                sent(rout.at[k, q], r_send.at[k, q])

            @pl.when(k < c - 1)
            def _():
                sent(rbout.at[k, q], rb_send.at[k, q])

            return 0

        lax.fori_loop(0, n_col, run, 0)

    each_chunk(finish)


def local(n_row, n_col, factors, right_side):
    tiles, rows, size = factors.shape
    width = right_side.shape[2]
    chunks = CHUNKS
    portion = width // chunks
    padded = -(-rows // 128) * 128
    column = lax.axis_index("col")
    row_index = lax.axis_index("row")

    tile_ids = jnp.arange(tiles)[:, None, None]
    global_rows = row_index * rows + jnp.arange(rows)[None, :, None]
    global_cols = jnp.arange(size)[None, None, :]
    lower = jnp.where(global_cols < global_rows, factors, 0.0) + (global_cols == global_rows).astype(jnp.float32)
    packed = jnp.where(tile_ids == column, lower, factors)
    diagonal = lax.dynamic_index_in_dim(factors, column, 0, keepdims=True)
    upper = jnp.where(global_cols >= global_rows, diagonal, 0.0)

    def arranged(a):
        a = a.reshape(a.shape[0], rows, n_row, rows).transpose(0, 2, 1, 3)
        return jnp.pad(a, ((0, 0), (0, 0), (0, padded - rows), (0, padded - rows)))

    whole = jnp.concatenate([arranged(packed), arranged(upper)], axis=0)
    high = lax.reduce_precision(whole, 8, 7)
    ahi = high.astype(jnp.bfloat16)
    alo = (whole - high).astype(jnp.bfloat16)

    rs = jnp.pad(right_side[0].T, ((0, 0), (0, padded - rows))).reshape(chunks, portion, padded)

    vmem = pl.BlockSpec(memory_space=pltpu.VMEM)
    anywhere = pl.BlockSpec(memory_space=pl.ANY)
    gathered = pltpu.VMEM((chunks, n_row, portion, padded), jnp.float32)
    staged = pltpu.VMEM((chunks, portion, padded), jnp.float32)
    runs = pltpu.VMEM((tiles, chunks, portion, padded), jnp.float32)
    weights = pltpu.VMEM((tiles + 1, n_row, padded, padded), jnp.bfloat16)
    dma = pltpu.SemaphoreType.DMA
    shape = jax.ShapeDtypeStruct((chunks, portion, padded), jnp.float32)
    fwd, sol = pl.pallas_call(
        functools.partial(kernel, n_row, n_col, chunks),
        out_shape=(shape, shape),
        in_specs=[anywhere, anywhere, vmem],
        out_specs=(vmem, vmem),
        scratch_shapes=[
            weights, weights, gathered, gathered, gathered, gathered, staged, staged, runs, runs, runs, runs,
            dma((2, tiles + 1)),
            *([dma((chunks, n_row))] * 8),
            *([dma((tiles, chunks))] * 4),
            dma((chunks,)),
        ],
        compiler_params=pltpu.CompilerParams(collective_id=0, has_side_effects=True, vmem_limit_bytes=60 << 20),
    )(ahi, alo, rs)

    def back(y):
        return y.reshape(width, padded)[:, :rows].T[None]

    return back(fwd), back(sol)


def solution(mesh):
    return jax.shard_map(
        functools.partial(local, mesh.shape["row"], mesh.shape["col"]),
        mesh=mesh,
        in_specs=(P("groups", "row", "col"), P(("groups", "col"), "row", None)),
        out_specs=(P(("groups", "col"), "row", None), P(("groups", "col"), "row", None)),
        check_vma=False,
    )
```

time: 549 us -> 139 us (0.25); the launches traced: 541 us -> 139 us
  blocking collectives: 285 us -> 0 us
  matrix products: 115 us -> 0 us
  Pallas kernels: 0 us -> 101 us
  waiting for transfers between devices: 34.9 us -> 0 us
  starting transfers between devices: 34.6 us -> 0 us
  local copies, waits for them, and re-layouts: 40.6 us -> 20.6 us
  other arithmetic: 28.5 us -> 16.1 us
    all_gather x20 -> x0, blocking collectives: 285 us -> none  [the longest x10 143 us: solve_tile(): lax.all_gather(pieces, 'row', axis=0, tiled=True)]
    dot_general x20 -> x0, matrix products: 115 us -> none  [product(): jnp.dot(left, right, preferred_element_type=jnp.float32, precision=precise)]
    pallas_call x0 -> x1, Pallas kernels: none -> 101 us  [local(): pl.pallas_call(functools.partial(kernel, n_row, n_col, chunks), out_shape...]
    ppermute x10 -> x0, waiting for transfers between devices: 34.9 us -> none  [from_behind(): return lax.ppermute(block, axis, route)]
    ppermute x10 -> x0, starting transfers between devices: 34.6 us -> none  [from_behind(): return lax.ppermute(block, axis, route)]
    while x20 -> x0, other arithmetic: 17 us -> none
    while x20 -> x0, local copies, waits for them, and re-layouts: 14.1 us -> none
    add x11 -> x1, other arithmetic: 9.63 us -> 0.01 us  [local(): global_rows = row_index * rows + jnp.arange(rows)[None, :, None]]
  transfers between devices with their start and end apart: 10 -> 0, of which waited for: 10 -> 0; matrix products, arithmetic and copies ran while one was open for 0% -> 0% of each run, Pallas kernels for 0% -> 0%
where the time goes in v1:
time: 139 us
  Pallas kernels  101 us (73%)
  local copies, waits for them, and re-layouts  20.6 us (15%)
  other arithmetic  16.1 us (12%)
    pallas_call x1, Pallas kernels, local(): pl.pallas_call(functools.partial(kernel, n_row, n_col, chunks), out_shape...  101 us
    reshape x4, local copies, waits for them, and re-layouts, arranged(): a = a.reshape(a.shape[0], rows, n_row, rows).transpose(0, 2, 1, 3)  18.2 us
    select_n x1, other arithmetic, local(): packed = jnp.where(tile_ids == column, lower, factors)  6.51 us
    convert_element_type x1, other arithmetic, local(): alo = (whole - high).astype(jnp.bfloat16)  6.42 us

profile of v1, /device:TPU:0, one launch (start us, length us, event | category | flops | bytes accessed | tf_op | source)
XLA Modules:
  0.0 138.7 jit_solution(16035871623598004258)
XLA Ops:
  0.6 2.8 %dynamic-slice_select_fusion = f32[1,320,1280]{2,1,0:T(8,128)} fusion(f32[4,320,1280]{2,1,0:T(8,128)} %param.2, s32[]{:T(128)S(6)} %select_n.18, s32[320]{0:T(512)S(1)} %iota_add_fusion), kind=kLoop, calls=%fused_computation.9 | loop fusion | flops 819200 | bytes 3278084 | tf_op jit(solution)/shard_map/jit(_where)/select_n | solution.py:280
  3.4 2.6 %reshape.106 = f32[1,320,4,320]{3,2,1,0:T(4,128)S(1)} reshape(f32[1,320,1280]{2,1,0:T(8,128)} %dynamic-slice_select_fusion) | data formatting | bytes 3276800 | tf_op jit(solution)/shard_map/reshape | solution.py:283
  6.0 1.4 %copy.9 = f32[1,320,4,320]{3,1,2,0:T(8,128)} copy(f32[1,320,4,320]{3,2,1,0:T(4,128)S(1)} %reshape.106) | data formatting | bytes 3276800 | tf_op jit(solution)/shard_map/reshape | solution.py:283
  7.5 0.4 iota_compare_fusion.4
  7.9 6.5 %add_select_fusion = f32[4,320,1280]{2,1,0:T(8,128)} fusion(f32[4,320,1280]{2,1,0:T(8,128)} %param.2, f32[320,1280]{1,0:T(8,128)S(1)} %get-tuple-element.9, pred[4]{0:T(512)(128)(4,1)S(1)} %iota_compare_fusion.5, pred[320,1280]{1,0:T(8,128)(4,1)S(1)} %get-tuple-element.8), kind=kLoop, calls=%fused_computation.7 | loop fusion | flops 4915200 | bytes 15155204 | tf_op jit(solution)/shard_map/jit(_where)/select_n | solution.py:278
  14.4 9.9 %reshape.105 = f32[4,320,4,320]{3,2,1,0:T(4,128)} reshape(f32[4,320,1280]{2,1,0:T(8,128)} %add_select_fusion) | data formatting | bytes 13107200 | tf_op jit(solution)/shard_map/reshape | solution.py:283
  24.3 0.0 copy-start
  24.3 4.3 %copy.8 = f32[4,320,4,320]{3,1,2,0:T(8,128)S(1)} copy(f32[4,320,4,320]{3,2,1,0:T(4,128)} %reshape.105) | data formatting | bytes 13107200 | tf_op jit(solution)/shard_map/reshape | solution.py:283
  28.6 0.0 copy-done
  28.6 0.0 copy-start.1
  28.6 6.4 %fusion = (bf16[5,4,384,384]{3,2,1,0:T(8,128)(2,1)}, bf16[5,4,384,384]{3,2,1,0:T(8,128)(2,1)}) fusion(f32[1,4,320,320]{3,2,1,0:T(8,128)S(1)} %bitcast.21, f32[4,4,320,320]{3,2,1,0:T(8,128)S(1)} %bitcast.20), kind=kLoop, calls=%fused_computation.2 | loop fusion | flops 26542080 | bytes 19988480 | tf_op jit(solution)/shard_map/convert_element_type | solution.py:289
  35.0 0.0 copy-done.1
  35.0 0.7 pad.14
  35.7 101.2 %shard_map.41 = (f32[3,32,384]{2,1,0:T(8,128)}, f32[3,32,384]{2,1,0:T(8,128)}) custom-call(bf16[5,4,384,384]{3,2,1,0:T(8,128)(2,1)} %get-tuple-element.7.ahi_hbm, bf16[5,4,384,384]{3,2,1,0:T(8,128)(2,1)} %get-tuple-element.6.alo_hbm, f32[3,32,384]{2,1,0:T(8,128)} %bitcast.22), custom_call_target="tpu_custom_call" | custom-call | tf_op jit(solution)/shard_map/pallas_call | solution.py:301
  137.0 1.7 %slice_bitcast_fusion = (f32[1,320,96]{1,2,0:T(8,128)}, f32[1,320,96]{1,2,0:T(8,128)}) fusion(f32[96,384]{1,0:T(8,128)} %bitcast.25, f32[96,384]{1,0:T(8,128)} %bitcast.24), kind=kLoop, calls=%fused_computation.14 | loop fusion | bytes 491520 | tf_op jit(solution)/shard_map/broadcast_in_dim | solution.py:317
  (2 shorter events, 0.0 us)
Async XLA Ops:
  24.3 4.3 %copy-start = (f32[1,320,4,320]{3,1,2,0:T(8,128)S(1)}, f32[1,320,4,320]{3,1,2,0:T(8,128)}, u32[]{:S(2)}) copy-start(f32[1,320,4,320]{3,1,2,0:T(8,128)} %copy.9) | copy-start | bytes 4915204
  28.6 6.4 %copy-start.1 = (f32[1,320,96]{1,2,0:T(8,128)S(1)}, f32[1,320,96]{1,2,0:T(8,128)}, u32[]{:S(2)}) copy-start(f32[1,320,96]{1,2,0:T(8,128)} %param.3) | copy-start | bytes 368644

commit v2 on v1

--- a/solution.py
+++ b/solution.py
@@ -12,34 +12,28 @@
 
 
 def kernel(
-    n_row, n_col, chunks,
-    ahi_hbm, alo_hbm, rs_ref,
+    n_row, n_col, chunks, rows, size, width, window, depth,
+    factors_hbm, rs_ref,
     fwd_ref, sol_ref,
-    ahi, alo, v_buf, f_buf, w_buf, s_buf, t_buf, tb_buf, rin, rout, rbin, rbout,
+    raw, ahi, alo, rs_pad, out_pad, rs_buf, v_buf, f_buf, w_buf, s_buf, t_buf, tb_buf, rin, rout, rbin, rbout,
     a_sem, v_send, v_recv, f_send, f_recv, w_send, w_recv, s_send, s_recv,
     r_send, r_recv, rb_send, rb_recv, b0_send,
 ):
     r = lax.axis_index("row")
     c = lax.axis_index("col")
     last = n_col - 1
-
-    def load(i, k):
-        return (
-            pltpu.make_async_copy(ahi_hbm.at[k], ahi.at[k], a_sem.at[0, k]),
-            pltpu.make_async_copy(alo_hbm.at[k], alo.at[k], a_sem.at[1, k]),
-        )
+    start = r * rows
+    shift = pl.multiple_of(start % 128, 8)
+
+    def load(k):
+        dst = raw.at[k, pl.ds(shift, rows), pl.ds(0, size)]
+        return pltpu.make_async_copy(factors_hbm.at[k], dst, a_sem.at[k])
 
     def start_load(i, _):
-        k = lax.rem(c + i, n_col + 1)
-        for copy in load(i, k):
-            copy.start()
+        load(lax.rem(c + i, n_col)).start()
         return 0
 
-    lax.fori_loop(0, n_col + 1, start_load, 0)
-
-    def wait_load(k):
-        for copy in load(0, k):
-            copy.wait()
+    lax.fori_loop(0, n_col, start_load, 0)
 
     barrier = pltpu.get_barrier_semaphore()
 
@@ -81,13 +75,14 @@
         lax.fori_loop(first, n_row, step, 0, unroll=n_row <= 4)
 
     def part(x, k, s):
+        columns = pl.ds(pl.multiple_of((s * rows) // 128 * 128, 128), window)
         hi = x.astype(jnp.bfloat16)
         lo = (x - hi.astype(jnp.float32)).astype(jnp.bfloat16)
         both = jnp.concatenate([hi, lo], axis=0)
         dims = (((1,), (1,)), ((), ()))
         m = x.shape[0]
-        one = lax.dot_general(both, ahi[k, s], dims, preferred_element_type=jnp.float32)
-        two = lax.dot_general(hi, alo[k, s], dims, preferred_element_type=jnp.float32)
+        one = lax.dot_general(both, ahi[k, :, columns], dims, preferred_element_type=jnp.float32)
+        two = lax.dot_general(hi, alo[k, :, columns], dims, preferred_element_type=jnp.float32)
         return one[:m] + one[m:] + two
 
     def combine(buf, k, q, wait):
@@ -119,22 +114,74 @@
     def to_row(src, buf, send, recv, q, row):
         return remote(src, buf.at[q, r], send.at[q, row], recv.at[q, r], row, c)
 
+    portion = width // chunks
+    rs_pad[...] = jnp.zeros(rs_pad.shape, jnp.float32)
+    rs_pad[pl.ds(shift, rows), :width] = rs_ref[0]
+    turned = rs_pad[...].T
+    for q in range(chunks):
+        rs_buf[q] = turned[q * portion : (q + 1) * portion]
+
+    def deliver(buf, out_ref):
+        whole = jnp.concatenate([buf[q, r] for q in range(chunks)], axis=0)
+        spare = out_pad.shape[1] - width
+        if spare:
+            whole = jnp.concatenate([whole, jnp.zeros((spare, window), jnp.float32)], axis=0)
+        out_pad[...] = whole.T
+        out_ref[0] = out_pad[pl.ds(shift, rows), :width]
+
     @pl.when(c == 0)
     def _():
         def one(q):
-            v_buf[q, r] = rs_ref[q]
-            each_row(lambda row: to_row(rs_ref.at[q], v_buf, v_send, v_recv, q, row).start(), 1)
+            v_buf[q, r] = rs_buf[q]
+            each_row(lambda row: to_row(rs_buf.at[q], v_buf, v_send, v_recv, q, row).start(), 1)
 
         each_chunk(one)
 
     def first_run(q):
-        return remote(rs_ref.at[q], rin.at[c, q], r_send.at[c, q], r_recv.at[c, q], r, 0)
+        return remote(rs_buf.at[q], rin.at[c, q], r_send.at[c, q], r_recv.at[c, q], r, 0)
 
     @pl.when(c > 0)
     def _():
         each_chunk(lambda q: first_run(q).start())
 
-    wait_load(c)
+    block = 16
+
+    def split(src, dst, kind):
+        def step(i, _):
+            base = pl.multiple_of(i * block, block)
+            line = lax.broadcasted_iota(jnp.int32, (block, depth), 0) + (base - shift)
+            place = lax.broadcasted_iota(jnp.int32, (block, depth), 1)
+            value = raw[src, pl.ds(base, block), :]
+            keep = (line >= 0) & (line < rows) & (place < size)
+            if kind == 1:
+                value = jnp.where(place == line + start, 1.0, value)
+                keep = keep & (place <= line + start)
+            if kind == 2:
+                keep = keep & (place >= line + start)
+            value = jnp.where(keep, value, 0.0)
+            hi = value.astype(jnp.bfloat16)
+            ahi[dst, pl.ds(base, block), :] = hi
+            alo[dst, pl.ds(base, block), :] = (value - hi.astype(jnp.float32)).astype(jnp.bfloat16)
+            return 0
+
+        lax.fori_loop(0, window // block, step, 0)
+
+    def split_others():
+        def step(i, _):
+            k = lax.rem(c + i, n_col)
+            load(k).wait()
+            split(k, k, 0)
+            return 0
+
+        lax.fori_loop(1, n_col, step, 0)
+        split(c, n_col, 2)
+
+    load(c).wait()
+    split(c, c, 1)
+
+    @pl.when(c > 0)
+    def _():
+        split_others()
 
     def back_run(q):
         return remote(f_buf.at[q, r], rbin.at[c, q], b0_send.at[q], rb_recv.at[c, q], r, last)
@@ -149,8 +196,6 @@
             def _():
                 back_run(q).start()
 
-            fwd_ref[q] = acc
-
         each_chunk(one)
 
     @pl.when(c == 0)
@@ -160,6 +205,12 @@
     @pl.when(c > 0)
     def _():
         solve_forward(arrival(v_buf, v_recv))
+
+    deliver(f_buf, fwd_ref)
+
+    @pl.when(c == 0)
+    def _():
+        split_others()
 
     def wait_run(run, recv, k, q):
         remote(run.at[k, q], run.at[k, q], recv.at[k, q], recv.at[k, q], r, c).wait_recv()
@@ -167,7 +218,6 @@
     def sweep(buf, recv, first, count, step, run_in, run_recv, run_out, run_send, stage, out, send, out_recv):
         nxt = c + step
         wait = arrival_but_own(buf, recv)
-        wait_load(first)
 
         def one(q):
             acc = combine(buf, first, q, wait)
@@ -181,7 +231,6 @@
 
         def other(i, _):
             k = first + step * i
-            wait_load(k)
 
             def inner(q):
                 acc = combine(buf, k, q, None)
@@ -198,7 +247,6 @@
     def _():
         sweep(f_buf, f_recv, c + 1, last - c, 1, rin, r_recv, rout, r_send, t_buf, v_buf, w_send, v_recv)
 
-    wait_load(n_col)
 
     def solve_backward(buf, wait):
         def one(q):
@@ -209,7 +257,6 @@
             def _():
                 each_row(lambda row: to_row(s_buf.at[q, r], s_buf, s_send, s_recv, q, row).start(), 1)
 
-            sol_ref[q] = acc
 
         each_chunk(one)
 
@@ -224,6 +271,8 @@
     @pl.when(c > 0)
     def _():
         sweep(s_buf, s_recv, c - 1, c, -1, rbin, rb_recv, rbout, rb_send, tb_buf, w_buf, v_send, w_recv)
+
+    deliver(s_buf, sol_ref)
 
     def sent(src, send):
         remote(src, src, send, send, r, c).wait_send()
@@ -231,11 +280,11 @@
     def finish(q):
         @pl.when(c == 0)
         def _():
-            each_row(lambda row: sent(rs_ref.at[q], v_send.at[q, row]), 1)
+            each_row(lambda row: sent(rs_buf.at[q], v_send.at[q, row]), 1)
 
         @pl.when(c > 0)
         def _():
-            sent(rs_ref.at[q], r_send.at[c, q])
+            sent(rs_buf.at[q], r_send.at[c, q])
             each_row(lambda row: sent(tb_buf.at[q], v_send.at[q, row]))
             each_row(lambda row: sent(s_buf.at[q, r], s_send.at[q, row]), 1)
 
@@ -267,56 +316,35 @@
     width = right_side.shape[2]
     chunks = CHUNKS
     portion = width // chunks
-    padded = -(-rows // 128) * 128
-    column = lax.axis_index("col")
-    row_index = lax.axis_index("row")
-
-    tile_ids = jnp.arange(tiles)[:, None, None]
-    global_rows = row_index * rows + jnp.arange(rows)[None, :, None]
-    global_cols = jnp.arange(size)[None, None, :]
-    lower = jnp.where(global_cols < global_rows, factors, 0.0) + (global_cols == global_rows).astype(jnp.float32)
-    packed = jnp.where(tile_ids == column, lower, factors)
-    diagonal = lax.dynamic_index_in_dim(factors, column, 0, keepdims=True)
-    upper = jnp.where(global_cols >= global_rows, diagonal, 0.0)
-
-    def arranged(a):
-        a = a.reshape(a.shape[0], rows, n_row, rows).transpose(0, 2, 1, 3)
-        return jnp.pad(a, ((0, 0), (0, 0), (0, padded - rows), (0, padded - rows)))
-
-    whole = jnp.concatenate([arranged(packed), arranged(upper)], axis=0)
-    high = lax.reduce_precision(whole, 8, 7)
-    ahi = high.astype(jnp.bfloat16)
-    alo = (whole - high).astype(jnp.bfloat16)
-
-    rs = jnp.pad(right_side[0].T, ((0, 0), (0, padded - rows))).reshape(chunks, portion, padded)
+    starts = [i * rows for i in range(n_row)]
+    window = max(-(-(i % 128 + rows) // 128) * 128 for i in starts)
+    depth = max(max(i // 128 * 128 + window for i in starts), size)
+    lanes = -(-width // 128) * 128
 
     vmem = pl.BlockSpec(memory_space=pltpu.VMEM)
     anywhere = pl.BlockSpec(memory_space=pl.ANY)
-    gathered = pltpu.VMEM((chunks, n_row, portion, padded), jnp.float32)
-    staged = pltpu.VMEM((chunks, portion, padded), jnp.float32)
-    runs = pltpu.VMEM((tiles, chunks, portion, padded), jnp.float32)
-    weights = pltpu.VMEM((tiles + 1, n_row, padded, padded), jnp.bfloat16)
+    gathered = pltpu.VMEM((chunks, n_row, portion, window), jnp.float32)
+    staged = pltpu.VMEM((chunks, portion, window), jnp.float32)
+    runs = pltpu.VMEM((tiles, chunks, portion, window), jnp.float32)
+    weights = pltpu.VMEM((tiles + 1, window, depth), jnp.bfloat16)
+    turning = pltpu.VMEM((window, lanes), jnp.float32)
     dma = pltpu.SemaphoreType.DMA
-    shape = jax.ShapeDtypeStruct((chunks, portion, padded), jnp.float32)
-    fwd, sol = pl.pallas_call(
-        functools.partial(kernel, n_row, n_col, chunks),
+    shape = jax.ShapeDtypeStruct(right_side.shape, jnp.float32)
+    return pl.pallas_call(
+        functools.partial(kernel, n_row, n_col, chunks, rows, size, width, window, depth),
         out_shape=(shape, shape),
-        in_specs=[anywhere, anywhere, vmem],
+        in_specs=[anywhere, vmem],
         out_specs=(vmem, vmem),
         scratch_shapes=[
-            weights, weights, gathered, gathered, gathered, gathered, staged, staged, runs, runs, runs, runs,
-            dma((2, tiles + 1)),
+            pltpu.VMEM((tiles, window, depth), jnp.float32), weights, weights, turning, turning, staged,
+            gathered, gathered, gathered, gathered, staged, staged, runs, runs, runs, runs,
+            dma((tiles,)),
             *([dma((chunks, n_row))] * 8),
             *([dma((tiles, chunks))] * 4),
             dma((chunks,)),
         ],
         compiler_params=pltpu.CompilerParams(collective_id=0, has_side_effects=True, vmem_limit_bytes=60 << 20),
-    )(ahi, alo, rs)
-
-    def back(y):
-        return y.reshape(width, padded)[:, :rows].T[None]
-
-    return back(fwd), back(sol)
+    )(factors, right_side)
 
 
 def solution(mesh):

time: 139 us -> 110 us (0.79)
  other arithmetic: 16.1 us -> 0 us
  local copies, waits for them, and re-layouts: 20.6 us -> 5.09 us
  Pallas kernels: 101 us -> 104 us
    reshape x4 -> x0, local copies, waits for them, and re-layouts: 18.2 us -> none  [arranged(): a = a.reshape(a.shape[0], rows, n_row, rows).transpose(0, 2, 1, 3)]
    select_n x2 -> x0, other arithmetic: 9.29 us -> none  [the longest x1 6.51 us: local(): packed = jnp.where(tile_ids == column, lower, factors)]
    convert_element_type x1 -> x0, other arithmetic: 6.42 us -> none  [local(): alo = (whole - high).astype(jnp.bfloat16)]
    pallas_call x0 -> x2, local copies, waits for them, and re-layouts: none -> 3.4 us  [local(): pl.pallas_call(functools.partial(kernel, n_row, n_col, chunks, rows, size...]
    pallas_call x1, Pallas kernels: 101 us -> 104 us  [local(): pl.pallas_call(functools.partial(kernel, n_row, n_col, chunks, rows, size...]
    broadcast_in_dim x1 -> x0, local copies, waits for them, and re-layouts: 1.71 us -> none  [back(): return y.reshape(width, padded)[:, :rows].T[None]]
    unnamed x4 -> x1, local copies, waits for them, and re-layouts: 0.01 us -> 1.69 us
where the time goes in v2:
time: 110 us
  Pallas kernels  104 us (95%)
  local copies, waits for them, and re-layouts  5.09 us (5%)
    pallas_call x1, Pallas kernels, local(): pl.pallas_call(functools.partial(kernel, n_row, n_col, chunks, rows, size...  104 us
    pallas_call x2, local copies, waits for them, and re-layouts, local(): pl.pallas_call(functools.partial(kernel, n_row, n_col, chunks, rows, size...  3.4 us

profile of v2, /device:TPU:0, one launch (start us, length us, event | category | flops | bytes accessed | tf_op | source)
XLA Modules:
  0.0 109.9 jit_solution(5192523171348855585)
XLA Ops:
  0.6 1.7 %copy.4.rs_ref = f32[1,320,96]{2,1,0:T(8,128)} copy(f32[1,320,96]{1,2,0:T(8,128)} %param.3) | data formatting | bytes 245760 | tf_op args[1]
  2.3 104.2 %shard_map.41 = (f32[1,320,96]{2,1,0:T(8,128)}, f32[1,320,96]{2,1,0:T(8,128)}) custom-call(f32[4,320,1280]{2,1,0:T(8,128)} %factors_hbm.1, f32[1,320,96]{2,1,0:T(8,128)} %copy.4.rs_ref), custom_call_target="tpu_custom_call" | custom-call | tf_op jit(solution)/shard_map/pallas_call | solution.py:333
  106.5 1.7 %copy.5 = f32[1,320,96]{1,2,0:T(8,128)} copy(f32[1,320,96]{2,1,0:T(8,128)} %get-tuple-element.2) | data formatting | bytes 245760 | tf_op jit(solution)/shard_map/pallas_call | solution.py:333
  108.2 1.7 %copy.6 = f32[1,320,96]{1,2,0:T(8,128)} copy(f32[1,320,96]{2,1,0:T(8,128)} %get-tuple-element.3) | data formatting | bytes 245760 | tf_op jit(solution)/shard_map/pallas_call | solution.py:333

commit v3 on v2

--- a/solution.py
+++ b/solution.py
@@ -8,7 +8,7 @@
 from jax.sharding import PartitionSpec as P
 
 MESH = pl.DeviceIdType.MESH
-CHUNKS = 3
+CHUNKS = 4
 
 
 def kernel(

time: 110 us -> 108 us (0.982)
  Pallas kernels: 104 us -> 102 us
    pallas_call x1, Pallas kernels: 104 us -> 102 us  [local(): pl.pallas_call(functools.partial(kernel, n_row, n_col, chunks, rows, size...]
where the time goes in v3:
time: 108 us
  Pallas kernels  102 us (94%)
  local copies, waits for them, and re-layouts  5.09 us (5%)
    pallas_call x1, Pallas kernels, local(): pl.pallas_call(functools.partial(kernel, n_row, n_col, chunks, rows, size...  102 us
    pallas_call x2, local copies, waits for them, and re-layouts, local(): pl.pallas_call(functools.partial(kernel, n_row, n_col, chunks, rows, size...  3.4 us

profile of v3, /device:TPU:0, one launch (start us, length us, event | category | flops | bytes accessed | tf_op | source)
XLA Modules:
  0.0 107.6 jit_solution(11284034681446316924)
XLA Ops:
  0.6 1.7 %copy.4.rs_ref = f32[1,320,96]{2,1,0:T(8,128)} copy(f32[1,320,96]{1,2,0:T(8,128)} %param.3) | data formatting | bytes 245760 | tf_op args[1]
  2.3 101.9 %shard_map.41 = (f32[1,320,96]{2,1,0:T(8,128)}, f32[1,320,96]{2,1,0:T(8,128)}) custom-call(f32[4,320,1280]{2,1,0:T(8,128)} %factors_hbm.1, f32[1,320,96]{2,1,0:T(8,128)} %copy.4.rs_ref), custom_call_target="tpu_custom_call" | custom-call | tf_op jit(solution)/shard_map/pallas_call | solution.py:333
  104.2 1.7 %copy.5 = f32[1,320,96]{1,2,0:T(8,128)} copy(f32[1,320,96]{2,1,0:T(8,128)} %get-tuple-element.2) | data formatting | bytes 245760 | tf_op jit(solution)/shard_map/pallas_call | solution.py:333
  105.9 1.7 %copy.6 = f32[1,320,96]{1,2,0:T(8,128)} copy(f32[1,320,96]{2,1,0:T(8,128)} %get-tuple-element.3) | data formatting | bytes 245760 | tf_op jit(solution)/shard_map/pallas_call | solution.py:333
